TPU v7x, 768 devices: a whole 4x8x12 slice. The times are simulated.
768 devices in a mesh: dp: 192 (over z_lo, x, y, core), seq: 4 (over z_hi).
Axes of the slice: x: 4, y: 8, z: 12 (z_hi: 4, z_lo: 3; z = z_hi * 3 + z_lo), core: 2. Of those that a mesh axis runs over, the one named last changes fastest.
Arguments:
- img_q_raw: bfloat16 [192, 512, 1536], P('dp', 'seq'), may hold values from -12 to 12
- img_k_raw: bfloat16 [192, 512, 1536], P('dp', 'seq'), may hold values from -6 to 6
- img_v: bfloat16 [192, 512, 1536], P('dp', 'seq'), may hold values from -6 to 6
- img_dout: bfloat16 [192, 512, 1536], P('dp', 'seq'), may hold values from -6 to 6
- txt_q_raw: bfloat16 [192, 64, 1536], P('dp', 'seq'), may hold values from -6 to 6
- txt_k_raw: bfloat16 [192, 64, 1536], P('dp'), may hold values from -6 to 6
- txt_v: bfloat16 [192, 64, 1536], P('dp'), may hold values from -6 to 6
- txt_dout: bfloat16 [192, 64, 1536], P('dp', 'seq'), may hold values from -6 to 6
- q_gain: float32 [128], replicated, may hold values from 0.6 to 3.8
- k_gain: float32 [128], replicated, may hold values from 0.6 to 3.8
Outputs:
- img_dq: bfloat16 [192, 512, 1536], P('dp', 'seq')
- img_dk: bfloat16 [192, 512, 1536], P('dp', 'seq')
- img_dv: bfloat16 [192, 512, 1536], P('dp', 'seq')
- txt_dq: bfloat16 [192, 64, 1536], P('dp', 'seq')
- txt_dk: bfloat16 [192, 64, 1536], P('dp', 'seq')
- txt_dv: bfloat16 [192, 64, 1536], P('dp', 'seq')
- q_gain_grad: float32 [128], replicated
- k_gain_grad: float32 [128], replicated
All inputs are finite; a program needn't handle non-finite values.
Results may differ from a plain program's by a relative error of at most 0.012.
The roundings to bfloat16 on the way count: a program that leaves them out, or rounds other values in their place, can miss the bound.
Values may be sent and summed in bfloat16 or wider, within the bound.
A program may use at most 64 MiB of HBM per device.

v0:
```python
import functools

import jax
import jax.numpy as jnp
from jax import lax
from jax.sharding import Mesh
from jax.sharding import PartitionSpec as P

HEAD_DIM = 128
DP_SEQ = ("dp_0", "dp_1", "dp_2", "dp_3", "seq")
DP = ("dp_0", "dp_1", "dp_2", "dp_3")


epsilon = 1e-06


def one_axis_at_a_time(x, axes):
    return functools.reduce(lax.psum, axes, x)


def normalize(source, norm_gain):
    values = source.astype(jnp.float32)
    inverse = lax.rsqrt(jnp.mean(values * values, axis=-1, keepdims=True) + epsilon)
    return values * inverse * norm_gain


def norm_backward(source, norm_gain, upstream):
    values = source.astype(jnp.float32)
    result_value, pullback = jax.vjp(normalize, values, norm_gain)
    return pullback(upstream)


def group_back(operands):
    query_b, key_b, value_all, dout_blocks = operands
    score_scale = query_b.shape[-1] ** (-0.5)
    scores = (
        jnp.einsum("nqhd,khd->nhqk", query_b, key_b, preferred_element_type=jnp.float32)
        * score_scale
    )
    row_max = jnp.max(scores, axis=-1, keepdims=True)
    shifted = scores - row_max
    log_total = jnp.log(jnp.sum(jnp.exp(shifted), axis=-1, keepdims=True))
    prob_full = jnp.exp(shifted - log_total)
    probs_b = prob_full.astype(jnp.bfloat16)
    output_b = jnp.einsum(
        "nhqk,khd->nqhd", probs_b, value_all, preferred_element_type=jnp.float32
    ).astype(jnp.bfloat16)
    output_b = lax.optimization_barrier(output_b)
    dprob = jnp.einsum("nqhd,khd->nhqk", dout_blocks, value_all, preferred_element_type=jnp.float32)
    row_delta = jnp.sum(dout_blocks.astype(jnp.float32) * output_b.astype(jnp.float32), axis=-1)
    row_delta = jnp.transpose(row_delta, (0, 2, 1))[..., None]
    dscore_b = (prob_full * (dprob - row_delta) * score_scale).astype(jnp.bfloat16)
    dquery = jnp.einsum("nhqk,khd->nqhd", dscore_b, key_b, preferred_element_type=jnp.float32)
    key_terms = jnp.einsum("nhqk,nqhd->nkhd", dscore_b, query_b, preferred_element_type=jnp.float32)
    value_terms = jnp.einsum(
        "nhqk,nqhd->nkhd", probs_b, dout_blocks, preferred_element_type=jnp.float32
    )
    return (dquery, key_terms, value_terms)


def forward_back(query_b, key_b, value_all, dout_blocks):
    block_count, query_rows, heads_here, feature_count = query_b.shape
    key_rows = key_b.shape[0]
    group_count = heads_here // heads_here

    def split_rows(source):
        return jnp.moveaxis(
            source.reshape(block_count, query_rows, group_count, heads_here, feature_count), 2, 0
        )

    def split_keys(source):
        return jnp.moveaxis(source.reshape(key_rows, group_count, heads_here, feature_count), 1, 0)

    dquery_g, key_g, value_g = lax.map(
        group_back,
        (split_rows(query_b), split_keys(key_b), split_keys(value_all), split_rows(dout_blocks)),
    )
    dquery = jnp.moveaxis(dquery_g, 0, 2).reshape(
        block_count, query_rows, heads_here, feature_count
    )
    key_terms = jnp.moveaxis(key_g, 0, 2).reshape(block_count, key_rows, heads_here, feature_count)
    value_terms = jnp.moveaxis(value_g, 0, 2).reshape(
        block_count, key_rows, heads_here, feature_count
    )
    return (dquery, key_terms, value_terms)


def local(
    img_q_raw, img_k_raw, img_v, img_dout, txt_q_raw, txt_k_raw, txt_v, txt_dout, q_gain, k_gain
):
    seq_count = lax.axis_size("seq")
    my_index = lax.axis_index("seq")
    image_q = img_q_raw[0]
    image_k = img_k_raw[0]
    image_v = img_v[0]
    image_d = img_dout[0]
    text_q = txt_q_raw[0]
    text_k = txt_k_raw[0]
    text_v = txt_v[0]
    text_d = txt_dout[0]
    lane_width = image_q.shape[1]
    head_count = lane_width // HEAD_DIM
    img_rows = image_q.shape[0]
    text_rows = text_q.shape[0]
    text_all = text_k.shape[0]
    image_total = img_rows * seq_count
    exchanged = (
        lax.all_to_all(image_q, "seq", split_axis=1, concat_axis=0, tiled=True),
        lax.all_to_all(image_k, "seq", split_axis=1, concat_axis=0, tiled=True),
        lax.all_to_all(image_v, "seq", split_axis=1, concat_axis=0, tiled=True),
        lax.all_to_all(image_d, "seq", split_axis=1, concat_axis=0, tiled=True),
        lax.all_to_all(text_q, "seq", split_axis=1, concat_axis=0, tiled=True),
        lax.all_to_all(text_d, "seq", split_axis=1, concat_axis=0, tiled=True),
    )
    moved_iq, moved_ik, moved_iv, moved_id, moved_tq, moved_td = exchanged
    local_heads = head_count // seq_count
    head_lanes = local_heads * HEAD_DIM
    key_text = lax.dynamic_slice_in_dim(text_k, my_index * head_lanes, head_lanes, 1)
    value_text = lax.dynamic_slice_in_dim(text_v, my_index * head_lanes, head_lanes, 1)
    query_src = jnp.concatenate(
        [
            moved_iq.reshape(seq_count, img_rows, local_heads, HEAD_DIM),
            moved_tq.reshape(seq_count, text_rows, local_heads, HEAD_DIM),
        ],
        axis=1,
    )
    dout_blocks = jnp.concatenate(
        [
            moved_id.reshape(seq_count, img_rows, local_heads, HEAD_DIM),
            moved_td.reshape(seq_count, text_rows, local_heads, HEAD_DIM),
        ],
        axis=1,
    )
    key_src = jnp.concatenate([moved_ik, key_text], axis=0).reshape(
        image_total + text_all, local_heads, HEAD_DIM
    )
    value_all = jnp.concatenate([moved_iv, value_text], axis=0).reshape(
        image_total + text_all, local_heads, HEAD_DIM
    )
    query_b = normalize(query_src, q_gain).astype(jnp.bfloat16)
    key_b = normalize(key_src, k_gain).astype(jnp.bfloat16)
    dquery, key_f, value_f = forward_back(query_b, key_b, value_all, dout_blocks)
    key_terms = key_f.astype(jnp.bfloat16)
    value_terms = value_f.astype(jnp.bfloat16)
    key_terms, value_terms = lax.optimization_barrier((key_terms, value_terms))
    dkey = jnp.sum(key_terms.astype(jnp.float32), axis=0)
    dvalue = jnp.sum(value_terms.astype(jnp.float32), axis=0)
    dquery_src, dq_gain = norm_backward(query_src, q_gain, dquery)
    dkey_src, dk_gain = norm_backward(key_src, k_gain, dkey)
    dq_b = dquery_src.astype(jnp.bfloat16)
    dk_b = dkey_src.reshape(image_total + text_all, head_lanes).astype(jnp.bfloat16)
    dv_b = dvalue.reshape(image_total + text_all, head_lanes).astype(jnp.bfloat16)
    returned = (
        dq_b[:, :img_rows].reshape(image_total, head_lanes),
        dk_b[:image_total],
        dv_b[:image_total],
        dq_b[:, img_rows:].reshape(text_all, head_lanes),
        dk_b[image_total:],
        dv_b[image_total:],
    )
    grad_iq, grad_ik, grad_iv, grad_tq, grad_tk, grad_tv = (
        lax.all_to_all(returned[0], "seq", split_axis=0, concat_axis=1, tiled=True),
        lax.all_to_all(returned[1], "seq", split_axis=0, concat_axis=1, tiled=True),
        lax.all_to_all(returned[2], "seq", split_axis=0, concat_axis=1, tiled=True),
        lax.all_to_all(returned[3], "seq", split_axis=0, concat_axis=1, tiled=True),
        lax.all_to_all(returned[4], "seq", split_axis=0, concat_axis=1, tiled=True),
        lax.all_to_all(returned[5], "seq", split_axis=0, concat_axis=1, tiled=True),
    )
    gain_q, gain_k = (one_axis_at_a_time(dq_gain, DP_SEQ), one_axis_at_a_time(dk_gain, DP_SEQ))
    return (
        grad_iq[None],
        grad_ik[None],
        grad_iv[None],
        grad_tq[None],
        grad_tk[None],
        grad_tv[None],
        gain_q,
        gain_k,
    )


def solution(mesh):
    finer = Mesh(
        mesh.devices.reshape(3, 4, 8, 2, mesh.shape["seq"]), ("dp_0", "dp_1", "dp_2", "dp_3", "seq")
    )
    placed = (
        P(DP, "seq", None),
        P(DP, "seq", None),
        P(DP, "seq", None),
        P(DP, "seq", None),
        P(DP, "seq", None),
        P(DP, None, None),
        P(DP, None, None),
        P(DP, "seq", None),
        P(),
        P(),
    )
    return jax.shard_map(
        local,
        mesh=finer,
        in_specs=placed,
        out_specs=(
            P(DP, "seq", None),
            P(DP, "seq", None),
            P(DP, "seq", None),
            P(DP, "seq", None),
            P(DP, "seq", None),
            P(DP, "seq", None),
            P(),
            P(),
        ),
        check_vma=False,
    )
```

profile of v0, /device:TPU:1, one launch (start us, length us, event | category | flops | bytes accessed | tf_op | source)
XLA Modules:
  0.0 286.5 jit_solution(18344631176782199521)
XLA Ops:
  2.2 15.0 %all-to-all-start.2 = ((bf16[16,4,384]{2,0,1:T(8,128)(2,1)}), bf16[16,4,384]{2,0,1:T(8,128)(2,1)S(1)}, u32[]{:S(2)}, u32[]{:S(2)}) async-start(bf16[16,4,384]{2,0,1:T(8,128)(2,1)} %copy.91), calls=%async_computation.2 | async-start | bytes 98304 | tf_op jit(solution)/shard_map/all_to_all | solution.py:112
  18.7 7.9 %all-to-all-done.2 = bf16[16,4,384]{2,0,1:T(8,128)(2,1)S(1)} async-done(((bf16[16,4,384]{2,0,1:T(8,128)(2,1)}), bf16[16,4,384]{2,0,1:T(8,128)(2,1)S(1)}, u32[]{:S(2)}, u32[]{:S(2)}) %all-to-all-start.2) | async-done | bytes 49184 | tf_op jit(solution)/shard_map/all_to_all | solution.py:112
  31.8 7.3 %all-to-all-done.5 = bf16[16,4,384]{2,0,1:T(8,128)(2,1)S(1)} async-done(((bf16[16,4,384]{2,0,1:T(8,128)(2,1)}), bf16[16,4,384]{2,0,1:T(8,128)(2,1)S(1)}, u32[]{:S(2)}, u32[]{:S(2)}) %all-to-all-start.5) | async-done | bytes 49184 | tf_op jit(solution)/shard_map/all_to_all | solution.py:113
  39.1 3.5 %all-to-all-start = ((bf16[128,4,384]{0,2,1:T(8,128)(2,1)}), bf16[128,4,384]{0,2,1:T(8,128)(2,1)S(1)}, u32[]{:S(2)}, u32[]{:S(2)}) async-start(bf16[128,4,384]{0,2,1:T(8,128)(2,1)} %bitcast), calls=%async_computation | async-start | bytes 786432 | tf_op jit(solution)/shard_map/all_to_all | solution.py:109
  44.5 9.6 %all-to-all-done = bf16[128,4,384]{0,2,1:T(8,128)(2,1)S(1)} async-done(((bf16[128,4,384]{0,2,1:T(8,128)(2,1)}), bf16[128,4,384]{0,2,1:T(8,128)(2,1)S(1)}, u32[]{:S(2)}, u32[]{:S(2)}) %all-to-all-start) | async-done | bytes 393248 | tf_op jit(solution)/shard_map/all_to_all | solution.py:109
  54.0 6.1 %all-to-all-start.1 = ((bf16[128,4,384]{0,2,1:T(8,128)(2,1)}), bf16[128,4,384]{0,2,1:T(8,128)(2,1)S(1)}, u32[]{:S(2)}, u32[]{:S(2)}) async-start(bf16[128,4,384]{0,2,1:T(8,128)(2,1)} %bitcast.4), calls=%async_computation.1 | async-start | bytes 786432 | tf_op jit(solution)/shard_map/all_to_all | solution.py:108
  64.3 7.1 %all-to-all-done.1 = bf16[128,4,384]{0,2,1:T(8,128)(2,1)S(1)} async-done(((bf16[128,4,384]{0,2,1:T(8,128)(2,1)}), bf16[128,4,384]{0,2,1:T(8,128)(2,1)S(1)}, u32[]{:S(2)}, u32[]{:S(2)}) %all-to-all-start.1) | async-done | bytes 393248 | tf_op jit(solution)/shard_map/all_to_all | solution.py:108
  71.4 3.5 %all-to-all-start.3 = ((bf16[128,4,384]{0,2,1:T(8,128)(2,1)}), bf16[128,4,384]{0,2,1:T(8,128)(2,1)S(1)}, u32[]{:S(2)}, u32[]{:S(2)}) async-start(bf16[128,4,384]{0,2,1:T(8,128)(2,1)} %bitcast.12), calls=%async_computation.3 | async-start | bytes 786432 | tf_op jit(solution)/shard_map/all_to_all | solution.py:110
  76.8 9.2 %all-to-all-done.3 = bf16[128,4,384]{0,2,1:T(8,128)(2,1)S(1)} async-done(((bf16[128,4,384]{0,2,1:T(8,128)(2,1)}), bf16[128,4,384]{0,2,1:T(8,128)(2,1)S(1)}, u32[]{:S(2)}, u32[]{:S(2)}) %all-to-all-start.3) | async-done | bytes 393248 | tf_op jit(solution)/shard_map/all_to_all | solution.py:110
  85.9 4.3 %all-to-all-start.4 = ((bf16[128,4,384]{0,2,1:T(8,128)(2,1)}), bf16[128,4,384]{0,2,1:T(8,128)(2,1)}, u32[]{:S(2)}, u32[]{:S(2)}) async-start(bf16[128,4,384]{0,2,1:T(8,128)(2,1)} %bitcast.14), calls=%async_computation.4 | async-start | bytes 786432 | tf_op jit(solution)/shard_map/all_to_all | solution.py:111
  97.8 7.7 %all-to-all-done.4 = bf16[128,4,384]{0,2,1:T(8,128)(2,1)} async-done(((bf16[128,4,384]{0,2,1:T(8,128)(2,1)}), bf16[128,4,384]{0,2,1:T(8,128)(2,1)}, u32[]{:S(2)}, u32[]{:S(2)}) %all-to-all-start.4) | async-done | bytes 393248 | tf_op jit(solution)/shard_map/all_to_all | solution.py:111
  123.2 3.5 %all-to-all-start.10 = ((bf16[4,16,384]{2,1,0:T(8,128)(2,1)}), bf16[4,16,384]{2,1,0:T(8,128)(2,1)S(1)}, u32[]{:S(2)}, u32[]{:S(2)}) async-start(bf16[4,16,384]{2,1,0:T(8,128)(2,1)} %bitcast.44), calls=%async_computation.10 | async-start | bytes 98304 | tf_op jit(solution)/shard_map/all_to_all | solution.py:166
  130.4 5.3 %all-to-all-done.10 = bf16[4,16,384]{2,1,0:T(8,128)(2,1)S(1)} async-done(((bf16[4,16,384]{2,1,0:T(8,128)(2,1)}), bf16[4,16,384]{2,1,0:T(8,128)(2,1)S(1)}, u32[]{:S(2)}, u32[]{:S(2)}) %all-to-all-start.10) | async-done | bytes 49184 | tf_op jit(solution)/shard_map/all_to_all | solution.py:166
  135.7 3.5 %all-to-all-start.11 = ((bf16[4,16,384]{2,1,0:T(8,128)(2,1)}), bf16[4,16,384]{2,1,0:T(8,128)(2,1)S(1)}, u32[]{:S(2)}, u32[]{:S(2)}) async-start(bf16[4,16,384]{2,1,0:T(8,128)(2,1)} %all_to_all.177), calls=%async_computation.11 | async-start | bytes 98304 | tf_op jit(solution)/shard_map/all_to_all | solution.py:167
  139.8 8.6 %all-to-all-done.11 = bf16[4,16,384]{2,1,0:T(8,128)(2,1)S(1)} async-done(((bf16[4,16,384]{2,1,0:T(8,128)(2,1)}), bf16[4,16,384]{2,1,0:T(8,128)(2,1)S(1)}, u32[]{:S(2)}, u32[]{:S(2)}) %all-to-all-start.11) | async-done | bytes 49184 | tf_op jit(solution)/shard_map/all_to_all | solution.py:167
  152.7 8.2 %all-to-all-done.9 = bf16[4,16,384]{2,1,0:T(8,128)(2,1)S(1)} async-done(((bf16[4,16,384]{2,1,0:T(8,128)(2,1)}), bf16[4,16,384]{2,1,0:T(8,128)(2,1)S(1)}, u32[]{:S(2)}, u32[]{:S(2)}) %all-to-all-start.9) | async-done | bytes 49184 | tf_op jit(solution)/shard_map/all_to_all | solution.py:165
  160.9 3.5 %all-to-all-start.7 = ((bf16[4,128,384]{2,1,0:T(8,128)(2,1)}), bf16[4,128,384]{2,1,0:T(8,128)(2,1)S(1)}, u32[]{:S(2)}, u32[]{:S(2)}) async-start(bf16[4,128,384]{2,1,0:T(8,128)(2,1)} %bitcast.38), calls=%async_computation.7 | async-start | bytes 786432 | tf_op jit(solution)/shard_map/all_to_all | solution.py:163
  165.4 10.0 %all-to-all-done.7 = bf16[4,128,384]{2,1,0:T(8,128)(2,1)S(1)} async-done(((bf16[4,128,384]{2,1,0:T(8,128)(2,1)}), bf16[4,128,384]{2,1,0:T(8,128)(2,1)S(1)}, u32[]{:S(2)}, u32[]{:S(2)}) %all-to-all-start.7) | async-done | bytes 393248 | tf_op jit(solution)/shard_map/all_to_all | solution.py:163
  179.9 10.0 %all-to-all-done.8 = bf16[4,128,384]{1,2,0:T(8,128)(2,1)S(1)} async-done(((bf16[4,128,384]{1,2,0:T(8,128)(2,1)}), bf16[4,128,384]{1,2,0:T(8,128)(2,1)S(1)}, u32[]{:S(2)}, u32[]{:S(2)}) %all-to-all-start.8) | async-done | bytes 393248 | tf_op jit(solution)/shard_map/all_to_all | solution.py:164
  193.4 23.3 %all-reduce.3 = (f32[128]{0:T(128)S(1)}, f32[128]{0:T(128)S(1)}) all-reduce(f32[128]{0:T(128)S(1)} %copy-done.20, f32[128]{0:T(128)S(1)} %copy-done.19), channel_id=1, replica_groups=mesh['dp_0'=3,'dp_1'=4,'dp_2'=8,'dp_3'=2,'seq'=4] {'dp_0'}, use_global_device_ids=true, to_apply=%region_10.11 | all-reduce | flops 256 | bytes 2048 | tf_op jit(solution)/shard_map/psum | solution.py:18
  216.7 9.0 %all-reduce.2 = (f32[128]{0:T(128)S(1)}, f32[128]{0:T(128)S(1)}) all-reduce(f32[128]{0:T(128)S(1)} %get-tuple-element.70, f32[128]{0:T(128)S(1)} %get-tuple-element.71), channel_id=1, replica_groups=mesh['dp_0'=3,'dp_1'=4,'dp_2'=8,'dp_3'=2,'seq'=4] {'dp_1'}, use_global_device_ids=true, to_apply=%region_11.12 | all-reduce | flops 256 | bytes 2048 | tf_op jit(solution)/shard_map/psum | solution.py:18
  225.8 13.9 %all-reduce = (f32[128]{0:T(128)S(1)}, f32[128]{0:T(128)S(1)}) all-reduce(f32[128]{0:T(128)S(1)} %get-tuple-element.68, f32[128]{0:T(128)S(1)} %get-tuple-element.69), channel_id=1, replica_groups=mesh['dp_0'=3,'dp_1'=4,'dp_2'=8,'dp_3'=2,'seq'=4] {'dp_2'}, use_global_device_ids=true, to_apply=%region_12.13 | all-reduce | flops 256 | bytes 2048 | tf_op jit(solution)/shard_map/psum | solution.py:18
  239.7 26.3 %all-reduce.4 = (f32[128]{0:T(128)S(1)}, f32[128]{0:T(128)S(1)}) all-reduce(f32[128]{0:T(128)S(1)} %get-tuple-element.64, f32[128]{0:T(128)S(1)} %get-tuple-element.65), channel_id=1, replica_groups=mesh['dp_0'=3,'dp_1'=4,'dp_2'=8,'dp_3'=2,'seq'=4] {'dp_3'}, use_global_device_ids=true, to_apply=%region_13.14 | all-reduce | flops 256 | bytes 2048 | tf_op jit(solution)/shard_map/psum | solution.py:18
  266.0 15.5 %all-reduce.1 = (f32[128]{0:T(128)}, f32[128]{0:T(128)}) all-reduce(f32[128]{0:T(128)S(1)} %get-tuple-element.72, f32[128]{0:T(128)S(1)} %get-tuple-element.73), channel_id=1, replica_groups=mesh['dp_0'=3,'dp_1'=4,'dp_2'=8,'dp_3'=2,'seq'=4] {'seq'}, use_global_device_ids=true, to_apply=%region_14.15 | all-reduce | flops 256 | bytes 2048 | tf_op jit(solution)/shard_map/psum | solution.py:18
  (127 shorter events, 63.5 us)
Async XLA Ops:
  0.6 61.8 %copy-start.6 = (bf16[1,128,1536]{2,1,0:T(8,128)(2,1)S(1)}, bf16[1,128,1536]{2,1,0:T(8,128)(2,1)}, u32[]{:S(2)}) copy-start(bf16[1,128,1536]{2,1,0:T(8,128)(2,1)} %param.12) | copy-start | bytes 1179652
  0.6 62.7 %copy-start.7 = (bf16[1,128,1536]{2,1,0:T(8,128)(2,1)S(1)}, bf16[1,128,1536]{2,1,0:T(8,128)(2,1)}, u32[]{:S(2)}) copy-start(bf16[1,128,1536]{2,1,0:T(8,128)(2,1)} %param.13) | copy-start | bytes 1179652
  0.7 63.7 %copy-start.15 = (f32[128]{0:T(128)S(1)}, f32[128]{0:T(128)}, u32[]{:S(2)}) copy-start(f32[128]{0:T(128)} %param.19) | copy-start | bytes 1540
  2.2 24.4 %all-to-all-start.2 = ((bf16[16,4,384]{2,0,1:T(8,128)(2,1)}), bf16[16,4,384]{2,0,1:T(8,128)(2,1)S(1)}, u32[]{:S(2)}, u32[]{:S(2)}) async-start(bf16[16,4,384]{2,0,1:T(8,128)(2,1)} %copy.91), calls=%async_computation.2 | async-start | bytes 98304 | tf_op jit(solution)/shard_map/all_to_all | solution.py:112
  26.6 12.5 %all-to-all-start.5 = ((bf16[16,4,384]{2,0,1:T(8,128)(2,1)}), bf16[16,4,384]{2,0,1:T(8,128)(2,1)S(1)}, u32[]{:S(2)}, u32[]{:S(2)}) async-start(bf16[16,4,384]{2,0,1:T(8,128)(2,1)} %copy.99), calls=%async_computation.5 | async-start | bytes 98304 | tf_op jit(solution)/shard_map/all_to_all | solution.py:113
  39.1 15.0 %all-to-all-start = ((bf16[128,4,384]{0,2,1:T(8,128)(2,1)}), bf16[128,4,384]{0,2,1:T(8,128)(2,1)S(1)}, u32[]{:S(2)}, u32[]{:S(2)}) async-start(bf16[128,4,384]{0,2,1:T(8,128)(2,1)} %bitcast), calls=%async_computation | async-start | bytes 786432 | tf_op jit(solution)/shard_map/all_to_all | solution.py:109
  54.0 21.6 %copy-start.3 = (bf16[128,4,384]{0,2,1:T(8,128)(2,1)}, bf16[128,4,384]{0,2,1:T(8,128)(2,1)S(1)}, u32[]{:S(2)}) copy-start(bf16[128,4,384]{0,2,1:T(8,128)(2,1)S(1)} %all-to-all-done) | copy-start | bytes 1179652
  54.0 17.4 %all-to-all-start.1 = ((bf16[128,4,384]{0,2,1:T(8,128)(2,1)}), bf16[128,4,384]{0,2,1:T(8,128)(2,1)S(1)}, u32[]{:S(2)}, u32[]{:S(2)}) async-start(bf16[128,4,384]{0,2,1:T(8,128)(2,1)} %bitcast.4), calls=%async_computation.1 | async-start | bytes 786432 | tf_op jit(solution)/shard_map/all_to_all | solution.py:108
  63.4 28.3 %copy-start.17 = (f32[128]{0:T(128)S(1)}, f32[128]{0:T(128)}, u32[]{:S(2)}) copy-start(f32[128]{0:T(128)} %param.18) | copy-start | bytes 1540
  71.4 14.5 %all-to-all-start.3 = ((bf16[128,4,384]{0,2,1:T(8,128)(2,1)}), bf16[128,4,384]{0,2,1:T(8,128)(2,1)S(1)}, u32[]{:S(2)}, u32[]{:S(2)}) async-start(bf16[128,4,384]{0,2,1:T(8,128)(2,1)} %bitcast.12), calls=%async_computation.3 | async-start | bytes 786432 | tf_op jit(solution)/shard_map/all_to_all | solution.py:110
  76.2 14.0 %copy-start.13 = (f32[576,3]{0,1:T(4,128)}, f32[576,3]{0,1:T(4,128)S(1)}, u32[]{:S(2)}) copy-start(f32[576,3]{0,1:T(4,128)S(1)} %fusion.29) | copy-start | bytes 20740
  76.7 13.5 %copy-start.12 = (f32[4,144,3]{1,0,2:T(4,128)}, f32[4,144,3]{1,0,2:T(4,128)S(1)}, u32[]{:S(2)}) copy-start(f32[4,144,3]{1,0,2:T(4,128)S(1)} %fusion.32) | copy-start | bytes 20740
  76.8 16.0 %copy-start.10 = (f32[4,144,3]{1,0,2:T(4,128)}, f32[4,144,3]{1,0,2:T(4,128)S(1)}, u32[]{:S(2)}) copy-start(f32[4,144,3]{1,0,2:T(4,128)S(1)} %fusion.42) | copy-start | bytes 20740
  85.9 19.6 %all-to-all-start.4 = ((bf16[128,4,384]{0,2,1:T(8,128)(2,1)}), bf16[128,4,384]{0,2,1:T(8,128)(2,1)}, u32[]{:S(2)}, u32[]{:S(2)}) async-start(bf16[128,4,384]{0,2,1:T(8,128)(2,1)} %bitcast.14), calls=%async_computation.4 | async-start | bytes 786432 | tf_op jit(solution)/shard_map/all_to_all | solution.py:111
  116.4 12.8 %copy-start = (bf16[4,576,3,128]{3,1,2,0:T(8,128)(2,1)S(1)}, bf16[4,576,3,128]{3,1,2,0:T(8,128)(2,1)}, u32[]{:S(2)}) copy-start(bf16[4,576,3,128]{3,1,2,0:T(8,128)(2,1)} %convert_bitcast_fusion) | copy-start | bytes 5308420
  123.2 12.4 %all-to-all-start.10 = ((bf16[4,16,384]{2,1,0:T(8,128)(2,1)}), bf16[4,16,384]{2,1,0:T(8,128)(2,1)S(1)}, u32[]{:S(2)}, u32[]{:S(2)}) async-start(bf16[4,16,384]{2,1,0:T(8,128)(2,1)} %bitcast.44), calls=%async_computation.10 | async-start | bytes 98304 | tf_op jit(solution)/shard_map/all_to_all | solution.py:166
  135.7 12.7 %all-to-all-start.11 = ((bf16[4,16,384]{2,1,0:T(8,128)(2,1)}), bf16[4,16,384]{2,1,0:T(8,128)(2,1)S(1)}, u32[]{:S(2)}, u32[]{:S(2)}) async-start(bf16[4,16,384]{2,1,0:T(8,128)(2,1)} %all_to_all.177), calls=%async_computation.11 | async-start | bytes 98304 | tf_op jit(solution)/shard_map/all_to_all | solution.py:167
  139.2 54.2 %copy-start.19 = (f32[128]{0:T(128)S(1)}, f32[128]{0:T(128)}, u32[]{:S(2)}) copy-start(f32[128]{0:T(128)} %get-tuple-element.60) | copy-start | bytes 1540
  139.2 54.2 %copy-start.20 = (f32[128]{0:T(128)S(1)}, f32[128]{0:T(128)}, u32[]{:S(2)}) copy-start(f32[128]{0:T(128)} %get-tuple-element.62) | copy-start | bytes 1540
  148.4 12.4 %all-to-all-start.9 = ((bf16[4,16,384]{2,1,0:T(8,128)(2,1)}), bf16[4,16,384]{2,1,0:T(8,128)(2,1)S(1)}, u32[]{:S(2)}, u32[]{:S(2)}) async-start(bf16[4,16,384]{2,1,0:T(8,128)(2,1)} %copy_bitcast_fusion), calls=%async_computation.9 | async-start | bytes 98304 | tf_op jit(solution)/shard_map/all_to_all | solution.py:165
  151.7 129.8 %copy-start.9 = (bf16[4,16,384]{2,1,0:T(8,128)(2,1)S(1)}, bf16[4,16,384]{2,1,0:T(8,128)(2,1)}, u32[]{:S(2)}) copy-start(bf16[4,16,384]{2,1,0:T(8,128)(2,1)} %copy-done.8) | copy-start | bytes 147460
  160.9 14.6 %all-to-all-start.7 = ((bf16[4,128,384]{2,1,0:T(8,128)(2,1)}), bf16[4,128,384]{2,1,0:T(8,128)(2,1)S(1)}, u32[]{:S(2)}, u32[]{:S(2)}) async-start(bf16[4,128,384]{2,1,0:T(8,128)(2,1)} %bitcast.38), calls=%async_computation.7 | async-start | bytes 786432 | tf_op jit(solution)/shard_map/all_to_all | solution.py:163
  175.4 14.5 %all-to-all-start.8 = ((bf16[4,128,384]{1,2,0:T(8,128)(2,1)}), bf16[4,128,384]{1,2,0:T(8,128)(2,1)S(1)}, u32[]{:S(2)}, u32[]{:S(2)}) async-start(bf16[4,128,384]{1,2,0:T(8,128)(2,1)} %copy.115), calls=%async_computation.8 | async-start | bytes 786432 | tf_op jit(solution)/shard_map/all_to_all | solution.py:164
  189.9 95.7 %all-to-all-start.6 = ((bf16[4,128,384]{1,2,0:T(8,128)(2,1)}), bf16[4,128,384]{1,2,0:T(8,128)(2,1)S(1)}, u32[]{:S(2)}, u32[]{:S(2)}) async-start(bf16[4,128,384]{1,2,0:T(8,128)(2,1)} %bitcast.27), calls=%async_computation.6 | async-start | bytes 786432 | tf_op jit(solution)/shard_map/all_to_all | solution.py:162
  (11 other events, 39.1 us)
where the time goes:
time: 288 us; the launch traced here: 286 us
  waiting for transfers between devices  90.8 us (32%)
  blocking collectives  88.1 us (31%)
  starting transfers between devices  56.3 us (20%)
  local copies, waits for them, and re-layouts  27.7 us (10%)
  other arithmetic  13.8 us (5%)
  matrix products  8.54 us (3%)
    psum x5, blocking collectives, one_axis_at_a_time(): return functools.reduce(lax.psum, axes, x)  88.1 us
    all_to_all x1, starting transfers between devices, local(): lax.all_to_all(text_q, 'seq', split_axis=1, concat_axis=0, tiled=True)  15 us
    all_to_all x1, waiting for transfers between devices, local(): lax.all_to_all(returned[2], 'seq', split_axis=0, concat_axis=1, tiled=True)  10 us
    all_to_all x1, waiting for transfers between devices, local(): lax.all_to_all(returned[1], 'seq', split_axis=0, concat_axis=1, tiled=True)  9.98 us
    all_to_all x1, waiting for transfers between devices, local(): lax.all_to_all(image_k, 'seq', split_axis=1, concat_axis=0, tiled=True)  9.59 us
    all_to_all x1, waiting for transfers between devices, local(): lax.all_to_all(image_v, 'seq', split_axis=1, concat_axis=0, tiled=True)  9.15 us
    unnamed x53, local copies, waits for them, and re-layouts  8.96 us
    all_to_all x1, waiting for transfers between devices, local(): lax.all_to_all(returned[5], 'seq', split_axis=0, concat_axis=1, tiled=True)  8.56 us
  transfers between devices with their start and end apart: 12, of which 11 were waited for; matrix products, arithmetic and copies ran while one was open for 10% of the time, Pallas kernels for 0%

commit v1 on v0

v1 whole, which is shorter than its diff:
```python
import functools

import jax
import jax.numpy as jnp
from jax import lax
from jax.experimental import pallas as pl
from jax.experimental.pallas import tpu as pltpu
from jax.sharding import PartitionSpec as P

HEAD_DIM = 128
EPSILON = 1e-06
DP_PARTS = (3, 4, 8, 2)
BF16 = jnp.bfloat16
F32 = jnp.float32


def axis_peers(part):
    stride = 1
    for size in DP_PARTS[part + 1 :]:
        stride *= size
    size = DP_PARTS[part]
    index = lax.axis_index("dp")
    place = lax.rem(index // stride, size)
    base = index - place * stride
    return [base + lax.rem(place + step, size) * stride for step in range(1, size)]


def dot_nt(a, b):
    return lax.dot_general(a, b, (((1,), (1,)), ((), ())), preferred_element_type=F32)


def dot_nn(a, b):
    return lax.dot_general(a, b, (((1,), (0,)), ((), ())), preferred_element_type=F32)


def dot_tn(a, b):
    return lax.dot_general(a, b, (((0,), (0,)), ((), ())), preferred_element_type=F32)


def inverse_rms(x):
    return lax.rsqrt(jnp.mean(x * x, axis=-1, keepdims=True) + EPSILON)


def norm_pull(x, gain, upstream):
    inverse = inverse_rms(x)
    unit = x * inverse
    scaled = upstream * gain
    along = jnp.mean(scaled * unit, axis=-1, keepdims=True)
    return inverse * (scaled - unit * along), upstream * unit


def exchange_kernel(
    seq_count,
    heads,
    img,
    txt,
    iq_ref,
    ik_ref,
    iv_ref,
    id_ref,
    tq_ref,
    tk_ref,
    tv_ref,
    td_ref,
    qg_ref,
    kg_ref,
    land_ref,
    gain_ref,
    stage,
    arrived,
    text_k,
    text_v,
    outgoing,
    keys,
    values,
    key_acc,
    value_acc,
    gain_src,
    gain_in,
    stage_sem,
    own_sem,
    in_send,
    in_recv,
    out_send,
    out_recv,
    own_out_sem,
    gain_send,
    gain_recv,
    gains,
):
    me = lax.axis_index("seq")
    rows = img + txt
    span = heads * HEAD_DIM
    scale = HEAD_DIM ** (-0.5)
    offsets = range(1, seq_count)
    seq_peers = [lax.rem(me + step, seq_count) for step in offsets]
    stages = [
        [{"seq": peer} for peer in seq_peers],
        [{"dp": peer} for peer in axis_peers(0)],
        [{"dp": peer} for peer in axis_peers(3)],
        [{"dp": peer} for peer in axis_peers(1)],
        [{"dp": peer} for peer in axis_peers(2)],
    ]
    barrier = pltpu.get_barrier_semaphore()
    total = 0
    for peers in stages:
        for peer in peers:
            pl.semaphore_signal(barrier, inc=1, device_id=peer, device_id_type=pl.DeviceIdType.MESH)
            total += 1

    def fetch(owner, target, sem):
        lanes = pl.ds(pl.multiple_of(owner * span, HEAD_DIM), span)
        row = 0
        for source, count in (
            (iq_ref, img),
            (tq_ref, txt),
            (id_ref, img),
            (td_ref, txt),
            (ik_ref, img),
            (iv_ref, img),
        ):
            pltpu.make_async_copy(
                source.at[0, :, lanes], target.at[pl.ds(row, count), :], sem
            ).start()
            row += count

    for step, peer in zip(offsets, seq_peers):
        fetch(peer, stage.at[step], stage_sem.at[step])
    fetch(me, stage.at[0], stage_sem.at[0])
    my_lanes = pl.ds(pl.multiple_of(me * span, HEAD_DIM), span)
    text_copies = (
        pltpu.make_async_copy(tk_ref.at[0, :, my_lanes], text_k, own_sem.at[0]),
        pltpu.make_async_copy(tv_ref.at[0, :, my_lanes], text_v, own_sem.at[1]),
        pltpu.make_async_copy(qg_ref, gains.at[pl.ds(0, 1)], own_sem.at[2]),
        pltpu.make_async_copy(kg_ref, gains.at[pl.ds(1, 1)], own_sem.at[3]),
    )
    for copy in text_copies:
        copy.start()

    def staged(step):
        return pltpu.make_async_copy(stage.at[step], stage.at[step], stage_sem.at[step])

    for step in offsets:
        staged(step).wait()
    pl.semaphore_wait(barrier, total)

    def in_copy(head, step):
        lanes = pl.ds(pl.multiple_of(head * HEAD_DIM, HEAD_DIM), HEAD_DIM)
        return pltpu.make_async_remote_copy(
            src_ref=stage.at[step, :, lanes],
            dst_ref=arrived.at[me, head],
            send_sem=in_send.at[head, step - 1],
            recv_sem=in_recv.at[head, step - 1],
            device_id={"seq": lax.rem(me + step, seq_count)},
            device_id_type=pl.DeviceIdType.MESH,
        )

    def out_copy(head, step):
        lanes = pl.ds(pl.multiple_of(head * HEAD_DIM, HEAD_DIM), HEAD_DIM)
        peer = lax.rem(me + step, seq_count)
        return pltpu.make_async_remote_copy(
            src_ref=outgoing.at[peer, head],
            dst_ref=land_ref.at[me, :, :, lanes],
            send_sem=out_send.at[head, step - 1],
            recv_sem=out_recv.at[head, step - 1],
            device_id={"seq": peer},
            device_id_type=pl.DeviceIdType.MESH,
        )

    def own_in(head):
        lanes = pl.ds(pl.multiple_of(head * HEAD_DIM, HEAD_DIM), HEAD_DIM)
        return pltpu.make_async_copy(
            stage.at[0, :, lanes], arrived.at[me, head], own_sem.at[4 + head]
        )

    def own_out(head):
        lanes = pl.ds(pl.multiple_of(head * HEAD_DIM, HEAD_DIM), HEAD_DIM)
        return pltpu.make_async_copy(
            outgoing.at[me, head], land_ref.at[me, :, :, lanes], own_out_sem.at[head]
        )

    def send_in(head, carry):
        for step in (2, 1, 3):
            in_copy(head, step).start()
        return carry

    lax.fori_loop(0, heads, send_in, 0)
    staged(0).wait()
    for copy in text_copies:
        copy.wait()

    def move_own(head, carry):
        own_in(head).start()
        return carry

    lax.fori_loop(0, heads, move_own, 0)
    q_gain = gains[0:1]
    k_gain = gains[1:2]
    do_row, k_row, v_row = rows, 2 * rows, 2 * rows + img

    def one_head(head, carry):
        q_total, k_total = carry
        own_in(head).wait()
        for step in offsets:
            in_copy(head, step).wait_recv()
        lanes = pl.ds(pl.multiple_of(head * HEAD_DIM, HEAD_DIM), HEAD_DIM)

        def raw_keys(j):
            return jnp.concatenate(
                [
                    arrived[j, head, k_row : k_row + img, :].astype(F32),
                    text_k[j * txt : (j + 1) * txt, lanes].astype(F32),
                ],
                axis=0,
            )

        for j in range(seq_count):
            x = raw_keys(j)
            keys[j] = (x * inverse_rms(x) * k_gain).astype(BF16)
            values[j, :img] = arrived[j, head, v_row : v_row + img, :]
            values[j, img:] = text_v[j * txt : (j + 1) * txt, lanes]
        kn = keys[...].reshape(seq_count * rows, HEAD_DIM)
        vv = values[...].reshape(seq_count * rows, HEAD_DIM)
        for j in range(seq_count):
            xq = arrived[j, head, :rows, :].astype(F32)
            qn = (xq * inverse_rms(xq) * q_gain).astype(BF16)
            dout = arrived[j, head, do_row : do_row + rows, :]
            scores = dot_nt(qn, kn) * scale
            weights = jnp.exp(scores - jnp.max(scores, axis=-1, keepdims=True))
            prob = weights * (1.0 / jnp.sum(weights, axis=-1, keepdims=True))
            prob_b = prob.astype(BF16)
            out_b = dot_nn(prob_b, vv).astype(BF16)
            delta = jnp.sum(dout.astype(F32) * out_b.astype(F32), axis=-1, keepdims=True)
            dscore = (prob * (dot_nt(dout, vv) - delta) * scale).astype(BF16)
            dq = dot_nn(dscore, kn)
            key_part = dot_tn(dscore, qn).astype(BF16).astype(F32)
            value_part = dot_tn(prob_b, dout).astype(BF16).astype(F32)
            if j == 0:
                key_acc[...] = key_part
                value_acc[...] = value_part
            else:
                key_acc[...] += key_part
                value_acc[...] += value_part
            dx, terms = norm_pull(xq, q_gain, dq)
            outgoing[j, head, 0] = dx.astype(BF16)
            q_total += jnp.sum(terms, axis=0, keepdims=True)
        for j in range(seq_count):
            dx, terms = norm_pull(raw_keys(j), k_gain, key_acc[j * rows : (j + 1) * rows])
            outgoing[j, head, 1] = dx.astype(BF16)
            outgoing[j, head, 2] = value_acc[j * rows : (j + 1) * rows].astype(BF16)
            k_total += jnp.sum(terms, axis=0, keepdims=True)

        @pl.when(head < heads - 1)
        def _():
            for step in (2, 1, 3):
                out_copy(head, step).start()
            own_out(head).start()

        return q_total, k_total

    zero = jnp.zeros((1, HEAD_DIM), F32)
    q_total, k_total = lax.fori_loop(0, heads, one_head, (zero, zero))
    gain = jnp.concatenate([q_total, k_total, jnp.zeros((6, HEAD_DIM), F32)], axis=0)
    slot = 0
    copies = []
    for number, peers in enumerate(stages):
        gain_src[number] = gain
        current = []
        for index, peer in enumerate(peers):
            copy = pltpu.make_async_remote_copy(
                src_ref=gain_src.at[number],
                dst_ref=gain_in.at[slot + index],
                send_sem=gain_send.at[slot + index],
                recv_sem=gain_recv.at[slot + index],
                device_id=peer,
                device_id_type=pl.DeviceIdType.MESH,
            )
            copy.start()
            current.append(copy)
        if number == 0:
            for step in (2, 1, 3):
                out_copy(heads - 1, step).start()
            own_out(heads - 1).start()
        for index, copy in enumerate(current):
            copy.wait_recv()
            gain = gain + gain_in[slot + index]
        copies += current
        slot += len(peers)
    gain_ref[...] = gain
    for copy in copies:
        copy.wait_send()

    def drain(head, carry):
        own_out(head).wait()
        for step in offsets:
            in_copy(head, step).wait_send()
            out_copy(head, step).wait()
        return carry

    lax.fori_loop(0, heads, drain, 0)


def place_kernel(seq_count, span, img, txt, land_ref, gain_ref, *refs):
    outs, sems = refs[:-1], refs[-1]
    copies = [(gain_ref.at[pl.ds(n, 1)], outs[6 + n]) for n in range(2)]
    for j in range(seq_count):
        lanes = pl.ds(j * span, span)
        for kind in range(3):
            copies.append((land_ref.at[j, kind, pl.ds(0, img)], outs[kind].at[0, :, lanes]))
            copies.append((land_ref.at[j, kind, pl.ds(img, txt)], outs[3 + kind].at[0, :, lanes]))
    started = [
        pltpu.make_async_copy(source, target, sems.at[number])
        for number, (source, target) in enumerate(copies)
    ]
    for copy in started:
        copy.start()
    for copy in started:
        copy.wait()


def local(seq_count, iq, ik, iv, idt, tq, tk, tv, td, q_gain, k_gain):
    img, lanes = iq.shape[1], iq.shape[2]
    txt = tq.shape[1]
    rows = img + txt
    heads = lanes // HEAD_DIM // seq_count
    span = heads * HEAD_DIM
    sent = 2 * rows + 2 * img
    peers = seq_count - 1 + sum(size - 1 for size in DP_PARTS)
    tokens = [
        pltpu.with_memory_space_constraint(x, pltpu.HBM)
        for x in (iq, ik, iv, idt, tq, tk, tv, td, q_gain[None], k_gain[None])
    ]
    hbm = pl.BlockSpec(memory_space=pltpu.HBM)
    vmem = pl.BlockSpec(memory_space=pltpu.VMEM)
    dma = pltpu.SemaphoreType.DMA
    land, gain = pl.pallas_call(
        functools.partial(exchange_kernel, seq_count, heads, img, txt),
        out_shape=(
            pltpu.VMEM((seq_count, 3, rows, span), BF16),
            pltpu.VMEM((8, HEAD_DIM), F32),
        ),
        in_specs=[hbm] * 10,
        out_specs=(vmem, vmem),
        scratch_shapes=[
            pltpu.VMEM((seq_count, sent, span), BF16),
            pltpu.VMEM((seq_count, heads, sent, HEAD_DIM), BF16),
            pltpu.VMEM((seq_count * txt, span), BF16),
            pltpu.VMEM((seq_count * txt, span), BF16),
            pltpu.VMEM((seq_count, heads, 3, rows, HEAD_DIM), BF16),
            pltpu.VMEM((seq_count, rows, HEAD_DIM), BF16),
            pltpu.VMEM((seq_count, rows, HEAD_DIM), BF16),
            pltpu.VMEM((seq_count * rows, HEAD_DIM), F32),
            pltpu.VMEM((seq_count * rows, HEAD_DIM), F32),
            pltpu.VMEM((1 + len(DP_PARTS), 8, HEAD_DIM), F32),
            pltpu.VMEM((peers, 8, HEAD_DIM), F32),
            dma((seq_count,)),
            dma((4 + heads,)),
            dma((heads, seq_count - 1)),
            dma((heads, seq_count - 1)),
            dma((heads, seq_count - 1)),
            dma((heads, seq_count - 1)),
            dma((heads,)),
            dma((peers,)),
            dma((peers,)),
            pltpu.VMEM((2, HEAD_DIM), F32),
        ],
        compiler_params=pltpu.CompilerParams(collective_id=0, has_side_effects=True, vmem_limit_bytes=40 << 20),
        name="exchange",
    )(*tokens)
    big = jax.ShapeDtypeStruct((1, img, lanes), BF16)
    small = jax.ShapeDtypeStruct((1, txt, lanes), BF16)
    row = jax.ShapeDtypeStruct((1, HEAD_DIM), F32)
    placed = pl.pallas_call(
        functools.partial(place_kernel, seq_count, span, img, txt),
        out_shape=(big,) * 3 + (small,) * 3 + (row,) * 2,
        in_specs=[vmem] * 2,
        out_specs=(hbm,) * 8,
        scratch_shapes=[dma((seq_count * 6 + 2,))],
        compiler_params=pltpu.CompilerParams(vmem_limit_bytes=4 << 20),
        name="place",
    )(*(pltpu.with_memory_space_constraint(x, pltpu.VMEM) for x in (land, gain)))
    return (*placed[:6], placed[6][0], placed[7][0])


def solution(mesh):
    split = P("dp", "seq", None)
    whole = P("dp", None, None)
    return jax.shard_map(
        functools.partial(local, mesh.shape["seq"]),
        mesh=mesh,
        in_specs=(split,) * 5 + (whole,) * 2 + (split, P(), P()),
        out_specs=(split,) * 6 + (P(), P()),
        check_vma=False,
    )
```

time: 288 us -> 129 us (0.45)
  Pallas kernels: 0 us -> 128 us
  waiting for transfers between devices: 90.8 us -> 0 us
  blocking collectives: 88.1 us -> 0 us
  starting transfers between devices: 56.3 us -> 0 us
  local copies, waits for them, and re-layouts: 27.7 us -> 0 us
  other arithmetic: 13.8 us -> 0 us
  matrix products: 8.54 us -> 0 us
    pallas_call x0 -> x2, Pallas kernels: none -> 128 us  [the longest x1 127 us: local(): pl.pallas_call(functools.partial(exchange_kernel, seq_count, heads, img,...]
    all_to_all x12 -> x0, waiting for transfers between devices: 90.8 us -> none  [the longest x1 10 us: local(): lax.all_to_all(returned[2], 'seq', split_axis=0, concat_axis=1, tiled=True)]
    psum x5 -> x0, blocking collectives: 88.1 us -> none  [one_axis_at_a_time(): return functools.reduce(lax.psum, axes, x)]
    all_to_all x12 -> x0, starting transfers between devices: 56.3 us -> none  [the longest x1 15 us: local(): lax.all_to_all(text_q, 'seq', split_axis=1, concat_axis=0, tiled=True)]
    unnamed x53 -> x0, local copies, waits for them, and re-layouts: 8.96 us -> none
    all_to_all x15 -> x0, local copies, waits for them, and re-layouts: 7.26 us -> none  [the longest x2 1.52 us: local(): lax.all_to_all(text_q, 'seq', split_axis=1, concat_axis=0, tiled=True)]
    dot_general x4 -> x0, matrix products: 6.99 us -> none  [the longest x1 2.54 us: group_back(): jnp.einsum('nhqk,khd->nqhd', dscore_b, key_b, preferred_element_type=jnp....]
    reduce_sum x7 -> x0, other arithmetic: 6.69 us -> none  [the longest x1 3.39 us: group_back(): log_total = jnp.log(jnp.sum(jnp.exp(shifted), axis=-1, keepdims=True))]
  transfers between devices with their start and end apart: 12 -> 0, of which waited for: 11 -> 0; matrix products, arithmetic and copies ran while one was open for 10% -> 0% of each run, Pallas kernels for 0% -> 0%
where the time goes in v1:
time: 129 us
  Pallas kernels  128 us (99%)
    pallas_call x1, Pallas kernels, local(): pl.pallas_call(functools.partial(exchange_kernel, seq_count, heads, img,...  127 us

profile of v1, /device:TPU:1, one launch (start us, length us, event | category | flops | bytes accessed | tf_op | source)
XLA Modules:
  0.0 128.5 jit_solution(6675258663887849)
XLA Ops:
  0.6 126.6 %exchange.1 = (bf16[4,3,144,384]{3,2,1,0:T(8,128)(2,1)S(1)}, f32[8,128]{1,0:T(8,128)S(1)}) custom-call(bf16[1,128,1536]{2,1,0:T(8,128)(2,1)} %iq_ref.1, bf16[1,128,1536]{2,1,0:T(8,128)(2,1)} %ik_ref.1, bf16[1,128,1536]{2,1,0:T(8,128)(2,1)} %iv_ref.1, bf16[1,128,1536]{2,1,0:T(8,128)(2,1)} %id_ref.1, bf16[1,16,1536]{2,1,0:T(8,128)(2,1)} %tq_ref.1, ...), custom_call_target="tpu_custom_call" | custom-call | tf_op jit(solution)/shard_map/exchange/pallas_call | solution.py:336
  127.2 1.3 place.1

commit v2 on v1

--- a/solution.py
+++ b/solution.py
@@ -22,7 +22,18 @@
     index = lax.axis_index("dp")
     place = lax.rem(index // stride, size)
     base = index - place * stride
-    return [base + lax.rem(place + step, size) * stride for step in range(1, size)]
+    return [{"dp": base + lax.rem(place + step, size) * stride} for step in range(1, size)]
+
+
+def column_peers(seq_count):
+    me = lax.axis_index("seq")
+    own = [{"dp": lax.axis_index("dp")}] + axis_peers(0)
+    return [
+        {**lower, "seq": lax.rem(me + step, seq_count)}
+        for step in range(seq_count)
+        for number, lower in enumerate(own)
+        if step or number
+    ]
 
 
 def dot_nt(a, b):
@@ -94,16 +105,10 @@
     scale = HEAD_DIM ** (-0.5)
     offsets = range(1, seq_count)
     seq_peers = [lax.rem(me + step, seq_count) for step in offsets]
-    stages = [
-        [{"seq": peer} for peer in seq_peers],
-        [{"dp": peer} for peer in axis_peers(0)],
-        [{"dp": peer} for peer in axis_peers(3)],
-        [{"dp": peer} for peer in axis_peers(1)],
-        [{"dp": peer} for peer in axis_peers(2)],
-    ]
+    stages = [axis_peers(3), axis_peers(1), axis_peers(2), column_peers(seq_count)]
     barrier = pltpu.get_barrier_semaphore()
     total = 0
-    for peers in stages:
+    for peers in reversed(stages):
         for peer in peers:
             pl.semaphore_signal(barrier, inc=1, device_id=peer, device_id_type=pl.DeviceIdType.MESH)
             total += 1
@@ -178,6 +183,12 @@
         return pltpu.make_async_copy(
             outgoing.at[me, head], land_ref.at[me, :, :, lanes], own_out_sem.at[head]
         )
+
+    def send_out(head):
+        for number in range(seq_count - 1):
+            peer = number + jnp.where(number >= me, 1, 0)
+            out_copy(head, lax.rem(peer - me + seq_count, seq_count)).start()
+        own_out(head).start()
 
     def send_in(head, carry):
         for step in (2, 1, 3):
@@ -252,15 +263,13 @@
 
         @pl.when(head < heads - 1)
         def _():
-            for step in (2, 1, 3):
-                out_copy(head, step).start()
-            own_out(head).start()
+            send_out(head)
 
         return q_total, k_total
 
     zero = jnp.zeros((1, HEAD_DIM), F32)
     q_total, k_total = lax.fori_loop(0, heads, one_head, (zero, zero))
-    gain = jnp.concatenate([q_total, k_total, jnp.zeros((6, HEAD_DIM), F32)], axis=0)
+    gain = jnp.concatenate([q_total, k_total], axis=0)
     slot = 0
     copies = []
     for number, peers in enumerate(stages):
@@ -277,10 +286,8 @@
             )
             copy.start()
             current.append(copy)
-        if number == 0:
-            for step in (2, 1, 3):
-                out_copy(heads - 1, step).start()
-            own_out(heads - 1).start()
+        if number == len(stages) - 1:
+            send_out(heads - 1)
         for index, copy in enumerate(current):
             copy.wait_recv()
             gain = gain + gain_in[slot + index]
@@ -325,7 +332,7 @@
     heads = lanes // HEAD_DIM // seq_count
     span = heads * HEAD_DIM
     sent = 2 * rows + 2 * img
-    peers = seq_count - 1 + sum(size - 1 for size in DP_PARTS)
+    peers = seq_count * DP_PARTS[0] - 1 + sum(size - 1 for size in DP_PARTS[1:])
     tokens = [
         pltpu.with_memory_space_constraint(x, pltpu.HBM)
         for x in (iq, ik, iv, idt, tq, tk, tv, td, q_gain[None], k_gain[None])
@@ -337,7 +344,7 @@
         functools.partial(exchange_kernel, seq_count, heads, img, txt),
         out_shape=(
             pltpu.VMEM((seq_count, 3, rows, span), BF16),
-            pltpu.VMEM((8, HEAD_DIM), F32),
+            pltpu.VMEM((2, HEAD_DIM), F32),
         ),
         in_specs=[hbm] * 10,
         out_specs=(vmem, vmem),
@@ -351,8 +358,8 @@
             pltpu.VMEM((seq_count, rows, HEAD_DIM), BF16),
             pltpu.VMEM((seq_count * rows, HEAD_DIM), F32),
             pltpu.VMEM((seq_count * rows, HEAD_DIM), F32),
-            pltpu.VMEM((1 + len(DP_PARTS), 8, HEAD_DIM), F32),
-            pltpu.VMEM((peers, 8, HEAD_DIM), F32),
+            pltpu.VMEM((len(DP_PARTS), 2, HEAD_DIM), F32),
+            pltpu.VMEM((peers, 2, HEAD_DIM), F32),
             dma((seq_count,)),
             dma((4 + heads,)),
             dma((heads, seq_count - 1)),

time: 129 us -> 119 us (0.922)
  the two profiles are of different devices: /device:TPU:1 before, /device:TPU:73 now
where the time goes in v2:
time: 119 us
  Pallas kernels  119 us (100%)
    pallas_call x1, Pallas kernels, local(): pl.pallas_call(functools.partial(exchange_kernel, seq_count, heads, img,...  117 us

profile of v2, /device:TPU:73, one launch (start us, length us, event | category | flops | bytes accessed | tf_op | source)
XLA Modules:
  0.0 119.3 jit_solution(1417859961271287811)
XLA Ops:
  0.6 117.3 %exchange.1 = (bf16[4,3,144,384]{3,2,1,0:T(8,128)(2,1)S(1)}, f32[2,128]{1,0:T(2,128)S(1)}) custom-call(bf16[1,128,1536]{2,1,0:T(8,128)(2,1)} %iq_ref.1, bf16[1,128,1536]{2,1,0:T(8,128)(2,1)} %ik_ref.1, bf16[1,128,1536]{2,1,0:T(8,128)(2,1)} %iv_ref.1, bf16[1,128,1536]{2,1,0:T(8,128)(2,1)} %id_ref.1, bf16[1,16,1536]{2,1,0:T(8,128)(2,1)} %tq_ref.1, ...), custom_call_target="tpu_custom_call" | custom-call | tf_op jit(solution)/shard_map/exchange/pallas_call | solution.py:343
  118.0 1.3 %place.1 = (bf16[1,128,1536]{2,1,0:T(8,128)(2,1)}, bf16[1,128,1536]{2,1,0:T(8,128)(2,1)}, bf16[1,128,1536]{2,1,0:T(8,128)(2,1)}, bf16[1,16,1536]{2,1,0:T(8,128)(...) custom-call(bf16[4,3,144,384]{3,2,1,0:T(8,128)(2,1)S(1)} %get-tuple-ele, ...), custom_call_target="tpu_custom_call" | custom-call | tf_op jit(solution)/shard_map/place/pallas_call | solution.py:380

commit v3 on v2

--- a/solution.py
+++ b/solution.py
@@ -9,7 +9,9 @@
 
 HEAD_DIM = 128
 EPSILON = 1e-06
+HELD = 3
 DP_PARTS = (3, 4, 8, 2)
+RINGS = (1, 2)
 BF16 = jnp.bfloat16
 F32 = jnp.float32
 
@@ -98,6 +100,7 @@
     gain_send,
     gain_recv,
     gains,
+    hello,
 ):
     me = lax.axis_index("seq")
     rows = img + txt
@@ -105,13 +108,12 @@
     scale = HEAD_DIM ** (-0.5)
     offsets = range(1, seq_count)
     seq_peers = [lax.rem(me + step, seq_count) for step in offsets]
-    stages = [axis_peers(3), axis_peers(1), axis_peers(2), column_peers(seq_count)]
+    stages = [column_peers(seq_count), axis_peers(3), axis_peers(1), axis_peers(2)]
+    near = [(axis_peers(part)[0], axis_peers(part)[-1]) for part in RINGS]
+    greeted = column_peers(seq_count) + axis_peers(3) + [peer for pair in near for peer in pair]
     barrier = pltpu.get_barrier_semaphore()
-    total = 0
-    for peers in reversed(stages):
-        for peer in peers:
-            pl.semaphore_signal(barrier, inc=1, device_id=peer, device_id_type=pl.DeviceIdType.MESH)
-            total += 1
+    for peer in greeted:
+        pl.semaphore_signal(barrier, inc=1, device_id=peer, device_id_type=pl.DeviceIdType.MESH)
 
     def fetch(owner, target, sem):
         lanes = pl.ds(pl.multiple_of(owner * span, HEAD_DIM), span)
@@ -147,7 +149,7 @@
 
     for step in offsets:
         staged(step).wait()
-    pl.semaphore_wait(barrier, total)
+    pl.semaphore_wait(barrier, len(greeted))
 
     def in_copy(head, step):
         lanes = pl.ds(pl.multiple_of(head * HEAD_DIM, HEAD_DIM), HEAD_DIM)
@@ -196,6 +198,15 @@
         return carry
 
     lax.fori_loop(0, heads, send_in, 0)
+    row = 0
+    for pair, part in zip(near, RINGS):
+        for _ in range(DP_PARTS[part] // 2 - 1):
+            for peer in pair:
+                pl.semaphore_signal(
+                    hello.at[row], inc=1, device_id=peer, device_id_type=pl.DeviceIdType.MESH
+                )
+            pl.semaphore_wait(hello.at[row], len(pair))
+            row += 1
     staged(0).wait()
     for copy in text_copies:
         copy.wait()
@@ -261,7 +272,7 @@
             outgoing[j, head, 2] = value_acc[j * rows : (j + 1) * rows].astype(BF16)
             k_total += jnp.sum(terms, axis=0, keepdims=True)
 
-        @pl.when(head < heads - 1)
+        @pl.when(head < heads - HELD)
         def _():
             send_out(head)
 
@@ -286,8 +297,9 @@
             )
             copy.start()
             current.append(copy)
-        if number == len(stages) - 1:
-            send_out(heads - 1)
+        if number == 0:
+            for head in range(heads - HELD, heads):
+                send_out(head)
         for index, copy in enumerate(current):
             copy.wait_recv()
             gain = gain + gain_in[slot + index]
@@ -370,6 +382,7 @@
             dma((peers,)),
             dma((peers,)),
             pltpu.VMEM((2, HEAD_DIM), F32),
+            pltpu.SemaphoreType.REGULAR((sum(DP_PARTS[part] // 2 - 1 for part in RINGS),)),
         ],
         compiler_params=pltpu.CompilerParams(collective_id=0, has_side_effects=True, vmem_limit_bytes=40 << 20),
         name="exchange",

time: 119 us -> 119 us (level)
  the two profiles are of different devices: /device:TPU:73 before, /device:TPU:1 now
where the time goes in v3:
time: 119 us; the launch traced here: 117 us
  Pallas kernels  116 us (97%)
    pallas_call x1, Pallas kernels, local(): pl.pallas_call(functools.partial(exchange_kernel, seq_count, heads, img,...  115 us

profile of v3, /device:TPU:1, one launch (start us, length us, event | category | flops | bytes accessed | tf_op | source)
XLA Modules:
  0.0 116.6 jit_solution(4750398935864536797)
XLA Ops:
  0.6 114.7 %exchange.1 = (bf16[4,3,144,384]{3,2,1,0:T(8,128)(2,1)S(1)}, f32[2,128]{1,0:T(2,128)S(1)}) custom-call(bf16[1,128,1536]{2,1,0:T(8,128)(2,1)} %iq_ref.1, bf16[1,128,1536]{2,1,0:T(8,128)(2,1)} %ik_ref.1, bf16[1,128,1536]{2,1,0:T(8,128)(2,1)} %iv_ref.1, bf16[1,128,1536]{2,1,0:T(8,128)(2,1)} %id_ref.1, bf16[1,16,1536]{2,1,0:T(8,128)(2,1)} %tq_ref.1, ...), custom_call_target="tpu_custom_call" | custom-call | tf_op jit(solution)/shard_map/exchange/pallas_call | solution.py:355
  115.3 1.3 %place.1 = (bf16[1,128,1536]{2,1,0:T(8,128)(2,1)}, bf16[1,128,1536]{2,1,0:T(8,128)(2,1)}, bf16[1,128,1536]{2,1,0:T(8,128)(2,1)}, bf16[1,16,1536]{2,1,0:T(8,128)(...) custom-call(bf16[4,3,144,384]{3,2,1,0:T(8,128)(2,1)S(1)} %get-tuple-ele, ...), custom_call_target="tpu_custom_call" | custom-call | tf_op jit(solution)/shard_map/place/pallas_call | solution.py:393

commit v4 on v3

--- a/solution.py
+++ b/solution.py
@@ -9,6 +9,7 @@
 
 HEAD_DIM = 128
 EPSILON = 1e-06
+LOG2E = 1.4426950408889634
 HELD = 3
 DP_PARTS = (3, 4, 8, 2)
 RINGS = (1, 2)
@@ -112,9 +113,6 @@
     near = [(axis_peers(part)[0], axis_peers(part)[-1]) for part in RINGS]
     greeted = column_peers(seq_count) + axis_peers(3) + [peer for pair in near for peer in pair]
     barrier = pltpu.get_barrier_semaphore()
-    for peer in greeted:
-        pl.semaphore_signal(barrier, inc=1, device_id=peer, device_id_type=pl.DeviceIdType.MESH)
-
     def fetch(owner, target, sem):
         lanes = pl.ds(pl.multiple_of(owner * span, HEAD_DIM), span)
         row = 0
@@ -131,8 +129,10 @@
             ).start()
             row += count
 
-    for step, peer in zip(offsets, seq_peers):
-        fetch(peer, stage.at[step], stage_sem.at[step])
+    for step in (2, 1, 3):
+        fetch(seq_peers[step - 1], stage.at[step], stage_sem.at[step])
+    for peer in greeted:
+        pl.semaphore_signal(barrier, inc=1, device_id=peer, device_id_type=pl.DeviceIdType.MESH)
     fetch(me, stage.at[0], stage_sem.at[0])
     my_lanes = pl.ds(pl.multiple_of(me * span, HEAD_DIM), span)
     text_copies = (
@@ -243,29 +243,48 @@
             values[j, img:] = text_v[j * txt : (j + 1) * txt, lanes]
         kn = keys[...].reshape(seq_count * rows, HEAD_DIM)
         vv = values[...].reshape(seq_count * rows, HEAD_DIM)
-        for j in range(seq_count):
+        def first_dots(j):
             xq = arrived[j, head, :rows, :].astype(F32)
             qn = (xq * inverse_rms(xq) * q_gain).astype(BF16)
             dout = arrived[j, head, do_row : do_row + rows, :]
-            scores = dot_nt(qn, kn) * scale
-            weights = jnp.exp(scores - jnp.max(scores, axis=-1, keepdims=True))
+            return qn, dot_nt(qn, kn), dot_nt(dout, vv)
+
+        def soften(scores):
+            weights = jnp.exp2((scores - jnp.max(scores, axis=-1, keepdims=True)) * (scale * LOG2E))
             prob = weights * (1.0 / jnp.sum(weights, axis=-1, keepdims=True))
-            prob_b = prob.astype(BF16)
+            return prob, prob.astype(BF16)
+
+        def score_gradient(j, prob, prob_b, dprob):
+            dout = arrived[j, head, do_row : do_row + rows, :]
             out_b = dot_nn(prob_b, vv).astype(BF16)
             delta = jnp.sum(dout.astype(F32) * out_b.astype(F32), axis=-1, keepdims=True)
-            dscore = (prob * (dot_nt(dout, vv) - delta) * scale).astype(BF16)
-            dq = dot_nn(dscore, kn)
+            return (prob * (dprob - delta) * scale).astype(BF16)
+
+        def value_terms(j, prob_b):
+            dout = arrived[j, head, do_row : do_row + rows, :]
+            value_part = dot_tn(prob_b, dout).astype(BF16).astype(F32)
+            value_acc[...] = value_part if j == 0 else value_acc[...] + value_part
+
+        def last_dots(j, qn, dscore):
             key_part = dot_tn(dscore, qn).astype(BF16).astype(F32)
-            value_part = dot_tn(prob_b, dout).astype(BF16).astype(F32)
-            if j == 0:
-                key_acc[...] = key_part
-                value_acc[...] = value_part
+            key_acc[...] = key_part if j == 0 else key_acc[...] + key_part
+            xq = arrived[j, head, :rows, :].astype(F32)
+            dx, terms = norm_pull(xq, q_gain, dot_nn(dscore, kn))
+            outgoing[j, head, 0] = dx.astype(BF16)
+            return jnp.sum(terms, axis=0, keepdims=True)
+
+        blocks, softs, dscores = {}, {}, {}
+        for step, j in (("first", 0), ("soft", 0), ("first", 1), ("score", 0), ("value", 0), ("soft", 1), ("first", 2), ("last", 0), ("score", 1), ("value", 1), ("soft", 2), ("first", 3), ("last", 1), ("score", 2), ("value", 2), ("soft", 3), ("last", 2), ("score", 3), ("value", 3), ("last", 3)):
+            if step == "first":
+                blocks[j] = first_dots(j)
+            elif step == "soft":
+                softs[j] = soften(blocks[j][1])
+            elif step == "score":
+                dscores[j] = score_gradient(j, *softs[j], blocks[j][2])
+            elif step == "value":
+                value_terms(j, softs[j][1])
             else:
-                key_acc[...] += key_part
-                value_acc[...] += value_part
-            dx, terms = norm_pull(xq, q_gain, dq)
-            outgoing[j, head, 0] = dx.astype(BF16)
-            q_total += jnp.sum(terms, axis=0, keepdims=True)
+                q_total += last_dots(j, blocks[j][0], dscores[j])
         for j in range(seq_count):
             dx, terms = norm_pull(raw_keys(j), k_gain, key_acc[j * rows : (j + 1) * rows])
             outgoing[j, head, 1] = dx.astype(BF16)

time: 119 us -> 118 us (level)
  no operation moved by 1% of the time
where the time goes in v4:
time: 118 us; the launch traced here: 116 us
  Pallas kernels  116 us (98%)
    pallas_call x1, Pallas kernels, local(): pl.pallas_call(functools.partial(exchange_kernel, seq_count, heads, img,...  114 us

profile of v4, /device:TPU:1, one launch (start us, length us, event | category | flops | bytes accessed | tf_op | source)
XLA Modules:
  0.0 116.3 jit_solution(17685284619509571747)
XLA Ops:
  0.6 114.4 %exchange.1 = (bf16[4,3,144,384]{3,2,1,0:T(8,128)(2,1)S(1)}, f32[2,128]{1,0:T(2,128)S(1)}) custom-call(bf16[1,128,1536]{2,1,0:T(8,128)(2,1)} %iq_ref.1, bf16[1,128,1536]{2,1,0:T(8,128)(2,1)} %ik_ref.1, bf16[1,128,1536]{2,1,0:T(8,128)(2,1)} %iv_ref.1, bf16[1,128,1536]{2,1,0:T(8,128)(2,1)} %id_ref.1, bf16[1,16,1536]{2,1,0:T(8,128)(2,1)} %tq_ref.1, ...), custom_call_target="tpu_custom_call" | custom-call | tf_op jit(solution)/shard_map/exchange/pallas_call | solution.py:374
  115.1 1.3 %place.1 = (bf16[1,128,1536]{2,1,0:T(8,128)(2,1)}, bf16[1,128,1536]{2,1,0:T(8,128)(2,1)}, bf16[1,128,1536]{2,1,0:T(8,128)(2,1)}, bf16[1,16,1536]{2,1,0:T(8,128)(...) custom-call(bf16[4,3,144,384]{3,2,1,0:T(8,128)(2,1)S(1)} %get-tuple-ele, ...), custom_call_target="tpu_custom_call" | custom-call | tf_op jit(solution)/shard_map/place/pallas_call | solution.py:412

commit v5 on v4

--- a/solution.py
+++ b/solution.py
@@ -61,6 +61,10 @@
     scaled = upstream * gain
     along = jnp.mean(scaled * unit, axis=-1, keepdims=True)
     return inverse * (scaled - unit * along), upstream * unit
+
+
+def wait_bytes(ref, sem):
+    pltpu.make_async_copy(ref, ref, sem).wait()
 
 
 def exchange_kernel(
@@ -133,6 +137,62 @@
         fetch(seq_peers[step - 1], stage.at[step], stage_sem.at[step])
     for peer in greeted:
         pl.semaphore_signal(barrier, inc=1, device_id=peer, device_id_type=pl.DeviceIdType.MESH)
+    def in_copy(head, step):
+        lanes = pl.ds(pl.multiple_of(head * HEAD_DIM, HEAD_DIM), HEAD_DIM)
+        return pltpu.make_async_remote_copy(
+            src_ref=stage.at[step, :, lanes],
+            dst_ref=arrived.at[me, head],
+            send_sem=in_send.at[0],
+            recv_sem=in_recv.at[head],
+            device_id={"seq": lax.rem(me + step, seq_count)},
+            device_id_type=pl.DeviceIdType.MESH,
+        )
+
+    def out_copy(head, step):
+        lanes = pl.ds(pl.multiple_of(head * HEAD_DIM, HEAD_DIM), HEAD_DIM)
+        peer = lax.rem(me + step, seq_count)
+        return pltpu.make_async_remote_copy(
+            src_ref=outgoing.at[peer, head],
+            dst_ref=land_ref.at[me, :, :, lanes],
+            send_sem=out_send.at[0],
+            recv_sem=out_recv.at[0],
+            device_id={"seq": peer},
+            device_id_type=pl.DeviceIdType.MESH,
+        )
+
+    def own_in(head):
+        lanes = pl.ds(pl.multiple_of(head * HEAD_DIM, HEAD_DIM), HEAD_DIM)
+        return pltpu.make_async_copy(
+            stage.at[0, :, lanes], arrived.at[me, head], own_sem.at[4 + head]
+        )
+
+    def own_out(head):
+        lanes = pl.ds(pl.multiple_of(head * HEAD_DIM, HEAD_DIM), HEAD_DIM)
+        return pltpu.make_async_copy(
+            outgoing.at[me, head], land_ref.at[me, :, :, lanes], own_out_sem.at[0]
+        )
+
+    def send_out(head):
+        for number in range(seq_count - 1):
+            peer = number + jnp.where(number >= me, 1, 0)
+            out_copy(head, lax.rem(peer - me + seq_count, seq_count)).start()
+        own_out(head).start()
+
+    def send_in(head, carry):
+        for step in (2, 1, 3):
+            in_copy(head, step).start()
+        return carry
+
+    def staged(step):
+        wait_bytes(stage.at[step], stage_sem.at[step])
+
+    staged(2)
+    pl.semaphore_wait(barrier, len(greeted))
+    in_copy(0, 2).start()
+    for step in (1, 3):
+        staged(step)
+        in_copy(0, step).start()
+    lax.fori_loop(1, heads, send_in, 0)
     fetch(me, stage.at[0], stage_sem.at[0])
     my_lanes = pl.ds(pl.multiple_of(me * span, HEAD_DIM), span)
     text_copies = (
@@ -144,60 +204,6 @@
     for copy in text_copies:
         copy.start()
 
-    def staged(step):
-        return pltpu.make_async_copy(stage.at[step], stage.at[step], stage_sem.at[step])
-
-    for step in offsets:
-        staged(step).wait()
-    pl.semaphore_wait(barrier, len(greeted))
-
-    def in_copy(head, step):
-        lanes = pl.ds(pl.multiple_of(head * HEAD_DIM, HEAD_DIM), HEAD_DIM)
-        return pltpu.make_async_remote_copy(
-            src_ref=stage.at[step, :, lanes],
-            dst_ref=arrived.at[me, head],
-            send_sem=in_send.at[head, step - 1],
-            recv_sem=in_recv.at[head, step - 1],
-            device_id={"seq": lax.rem(me + step, seq_count)},
-            device_id_type=pl.DeviceIdType.MESH,
-        )
-
-    def out_copy(head, step):
-        lanes = pl.ds(pl.multiple_of(head * HEAD_DIM, HEAD_DIM), HEAD_DIM)
-        peer = lax.rem(me + step, seq_count)
-        return pltpu.make_async_remote_copy(
-            src_ref=outgoing.at[peer, head],
-            dst_ref=land_ref.at[me, :, :, lanes],
-            send_sem=out_send.at[head, step - 1],
-            recv_sem=out_recv.at[head, step - 1],
-            device_id={"seq": peer},
-            device_id_type=pl.DeviceIdType.MESH,
-        )
-
-    def own_in(head):
-        lanes = pl.ds(pl.multiple_of(head * HEAD_DIM, HEAD_DIM), HEAD_DIM)
-        return pltpu.make_async_copy(
-            stage.at[0, :, lanes], arrived.at[me, head], own_sem.at[4 + head]
-        )
-
-    def own_out(head):
-        lanes = pl.ds(pl.multiple_of(head * HEAD_DIM, HEAD_DIM), HEAD_DIM)
-        return pltpu.make_async_copy(
-            outgoing.at[me, head], land_ref.at[me, :, :, lanes], own_out_sem.at[head]
-        )
-
-    def send_out(head):
-        for number in range(seq_count - 1):
-            peer = number + jnp.where(number >= me, 1, 0)
-            out_copy(head, lax.rem(peer - me + seq_count, seq_count)).start()
-        own_out(head).start()
-
-    def send_in(head, carry):
-        for step in (2, 1, 3):
-            in_copy(head, step).start()
-        return carry
-
-    lax.fori_loop(0, heads, send_in, 0)
     row = 0
     for pair, part in zip(near, RINGS):
         for _ in range(DP_PARTS[part] // 2 - 1):
@@ -207,7 +213,7 @@
                 )
             pl.semaphore_wait(hello.at[row], len(pair))
             row += 1
-    staged(0).wait()
+    staged(0)
     for copy in text_copies:
         copy.wait()
 
@@ -223,8 +229,7 @@
     def one_head(head, carry):
         q_total, k_total = carry
         own_in(head).wait()
-        for step in offsets:
-            in_copy(head, step).wait_recv()
+        wait_bytes(arrived.at[pl.ds(0, seq_count - 1), head], in_recv.at[head])
         lanes = pl.ds(pl.multiple_of(head * HEAD_DIM, HEAD_DIM), HEAD_DIM)
 
         def raw_keys(j):
@@ -301,59 +306,46 @@
     q_total, k_total = lax.fori_loop(0, heads, one_head, (zero, zero))
     gain = jnp.concatenate([q_total, k_total], axis=0)
     slot = 0
-    copies = []
     for number, peers in enumerate(stages):
         gain_src[number] = gain
-        current = []
         for index, peer in enumerate(peers):
             copy = pltpu.make_async_remote_copy(
                 src_ref=gain_src.at[number],
                 dst_ref=gain_in.at[slot + index],
-                send_sem=gain_send.at[slot + index],
-                recv_sem=gain_recv.at[slot + index],
+                send_sem=gain_send.at[0],
+                recv_sem=gain_recv.at[number],
                 device_id=peer,
                 device_id_type=pl.DeviceIdType.MESH,
             )
             copy.start()
-            current.append(copy)
         if number == 0:
             for head in range(heads - HELD, heads):
                 send_out(head)
-        for index, copy in enumerate(current):
-            copy.wait_recv()
+        wait_bytes(gain_in.at[pl.ds(slot, len(peers))], gain_recv.at[number])
+        for index in range(len(peers)):
             gain = gain + gain_in[slot + index]
-        copies += current
         slot += len(peers)
     gain_ref[...] = gain
-    for copy in copies:
-        copy.wait_send()
-
-    def drain(head, carry):
-        own_out(head).wait()
-        for step in offsets:
-            in_copy(head, step).wait_send()
-            out_copy(head, step).wait()
-        return carry
-
-    lax.fori_loop(0, heads, drain, 0)
+    wait_bytes(gain_in, gain_send.at[0])
+    wait_bytes(arrived.at[pl.ds(0, seq_count - 1)], in_send.at[0])
+    wait_bytes(outgoing.at[0], own_out_sem.at[0])
+    wait_bytes(outgoing.at[pl.ds(0, seq_count - 1)], out_send.at[0])
+    wait_bytes(outgoing.at[pl.ds(0, seq_count - 1)], out_recv.at[0])
 
 
 def place_kernel(seq_count, span, img, txt, land_ref, gain_ref, *refs):
     outs, sems = refs[:-1], refs[-1]
-    copies = [(gain_ref.at[pl.ds(n, 1)], outs[6 + n]) for n in range(2)]
     for j in range(seq_count):
         lanes = pl.ds(j * span, span)
         for kind in range(3):
-            copies.append((land_ref.at[j, kind, pl.ds(0, img)], outs[kind].at[0, :, lanes]))
-            copies.append((land_ref.at[j, kind, pl.ds(img, txt)], outs[3 + kind].at[0, :, lanes]))
-    started = [
-        pltpu.make_async_copy(source, target, sems.at[number])
-        for number, (source, target) in enumerate(copies)
-    ]
-    for copy in started:
-        copy.start()
-    for copy in started:
-        copy.wait()
+            for out, first, count in ((outs[kind], 0, img), (outs[3 + kind], img, txt)):
+                pltpu.make_async_copy(
+                    land_ref.at[j, kind, pl.ds(first, count)], out.at[0, :, lanes], sems.at[0]
+                ).start()
+    for n in range(2):
+        pltpu.make_async_copy(gain_ref.at[pl.ds(n, 1)], outs[6 + n], sems.at[1]).start()
+    wait_bytes(land_ref, sems.at[0])
+    wait_bytes(gain_ref, sems.at[1])
 
 
 def local(seq_count, iq, ik, iv, idt, tq, tk, tv, td, q_gain, k_gain):
@@ -393,13 +385,13 @@
             pltpu.VMEM((peers, 2, HEAD_DIM), F32),
             dma((seq_count,)),
             dma((4 + heads,)),
-            dma((heads, seq_count - 1)),
-            dma((heads, seq_count - 1)),
-            dma((heads, seq_count - 1)),
-            dma((heads, seq_count - 1)),
+            dma((1,)),
             dma((heads,)),
-            dma((peers,)),
-            dma((peers,)),
+            dma((1,)),
+            dma((1,)),
+            dma((1,)),
+            dma((1,)),
+            dma((len(DP_PARTS),)),
             pltpu.VMEM((2, HEAD_DIM), F32),
             pltpu.SemaphoreType.REGULAR((sum(DP_PARTS[part] // 2 - 1 for part in RINGS),)),
         ],
@@ -414,7 +406,7 @@
         out_shape=(big,) * 3 + (small,) * 3 + (row,) * 2,
         in_specs=[vmem] * 2,
         out_specs=(hbm,) * 8,
-        scratch_shapes=[dma((seq_count * 6 + 2,))],
+        scratch_shapes=[dma((2,))],
         compiler_params=pltpu.CompilerParams(vmem_limit_bytes=4 << 20),
         name="place",
     )(*(pltpu.with_memory_space_constraint(x, pltpu.VMEM) for x in (land, gain)))

time: 118 us -> 117 us (level)
  no operation moved by 1% of the time
where the time goes in v5:
time: 117 us; the launch traced here: 115 us
  Pallas kernels  115 us (98%)
    pallas_call x1, Pallas kernels, local(): pl.pallas_call(functools.partial(exchange_kernel, seq_count, heads, img,...  114 us

profile of v5, /device:TPU:1, one launch (start us, length us, event | category | flops | bytes accessed | tf_op | source)
XLA Modules:
  0.0 115.4 jit_solution(6632329670037121687)
XLA Ops:
  0.6 113.7 %exchange.1 = (bf16[4,3,144,384]{3,2,1,0:T(8,128)(2,1)S(1)}, f32[2,128]{1,0:T(2,128)S(1)}) custom-call(bf16[1,128,1536]{2,1,0:T(8,128)(2,1)} %iq_ref.1, bf16[1,128,1536]{2,1,0:T(8,128)(2,1)} %ik_ref.1, bf16[1,128,1536]{2,1,0:T(8,128)(2,1)} %iv_ref.1, bf16[1,128,1536]{2,1,0:T(8,128)(2,1)} %id_ref.1, bf16[1,16,1536]{2,1,0:T(8,128)(2,1)} %tq_ref.1, ...), custom_call_target="tpu_custom_call" | custom-call | tf_op jit(solution)/shard_map/exchange/pallas_call | solution.py:366
  114.4 1.1 place.1

commit v6 on v5

--- a/solution.py
+++ b/solution.py
@@ -10,7 +10,6 @@
 HEAD_DIM = 128
 EPSILON = 1e-06
 LOG2E = 1.4426950408889634
-HELD = 3
 DP_PARTS = (3, 4, 8, 2)
 RINGS = (1, 2)
 BF16 = jnp.bfloat16
@@ -172,11 +171,18 @@
             outgoing.at[me, head], land_ref.at[me, :, :, lanes], own_out_sem.at[0]
         )
 
-    def send_out(head):
-        for number in range(seq_count - 1):
-            peer = number + jnp.where(number >= me, 1, 0)
-            out_copy(head, lax.rem(peer - me + seq_count, seq_count)).start()
-        own_out(head).start()
+    def send_out():
+        half = seq_count // 2
+        for group in (range(half), range(half, seq_count)):
+            for head in range(heads):
+                for peer in group:
+
+                    @pl.when(me != peer)
+                    def _(head=head, peer=peer):
+                        out_copy(head, lax.rem(peer - me + seq_count, seq_count)).start()
+
+        for head in range(heads):
+            own_out(head).start()
 
     def send_in(head, carry):
         for step in (2, 1, 3):
@@ -296,10 +302,6 @@
             outgoing[j, head, 2] = value_acc[j * rows : (j + 1) * rows].astype(BF16)
             k_total += jnp.sum(terms, axis=0, keepdims=True)
 
-        @pl.when(head < heads - HELD)
-        def _():
-            send_out(head)
-
         return q_total, k_total
 
     zero = jnp.zeros((1, HEAD_DIM), F32)
@@ -319,8 +321,7 @@
             )
             copy.start()
         if number == 0:
-            for head in range(heads - HELD, heads):
-                send_out(head)
+            send_out()
         wait_bytes(gain_in.at[pl.ds(slot, len(peers))], gain_recv.at[number])
         for index in range(len(peers)):
             gain = gain + gain_in[slot + index]

time: 117 us -> 117 us (level)
  no operation moved by 1% of the time
where the time goes in v6:
time: 117 us; the launch traced here: 115 us
  Pallas kernels  114 us (97%)
    pallas_call x1, Pallas kernels, local(): pl.pallas_call(functools.partial(exchange_kernel, seq_count, heads, img,...  113 us

profile of v6, /device:TPU:1, one launch (start us, length us, event | category | flops | bytes accessed | tf_op | source)
XLA Modules:
  0.0 115.1 jit_solution(1995998719933114137)
XLA Ops:
  0.6 113.4 %exchange.1 = (bf16[4,3,144,384]{3,2,1,0:T(8,128)(2,1)S(1)}, f32[2,128]{1,0:T(2,128)S(1)}) custom-call(bf16[1,128,1536]{2,1,0:T(8,128)(2,1)} %iq_ref.1, bf16[1,128,1536]{2,1,0:T(8,128)(2,1)} %ik_ref.1, bf16[1,128,1536]{2,1,0:T(8,128)(2,1)} %iv_ref.1, bf16[1,128,1536]{2,1,0:T(8,128)(2,1)} %id_ref.1, bf16[1,16,1536]{2,1,0:T(8,128)(2,1)} %tq_ref.1, ...), custom_call_target="tpu_custom_call" | custom-call | tf_op jit(solution)/shard_map/exchange/pallas_call | solution.py:367
  114.0 1.1 place.1
